TPU v7x, 32 devices: a whole 2x2x4 slice. The times are simulated.
32 devices in a mesh: tm: 8 (over z, x), mp: 4 (over y, core).
Axes of the slice: x: 2, y: 2, z: 4, core: 2. Of those that a mesh axis runs over, the one named last changes fastest.
Arguments:
- features: bfloat16 [256, 2048], P('tm'), may hold values from -6 to 6
- w_in: bfloat16 [2048, 4096], P(None, 'mp'), may hold values from -0.125 to 0.125
- b_in: float32 [4096], P('mp'), may hold values from -5 to 5
- output_weight: bfloat16 [4096, 256], P('mp'), may hold values from -0.09375 to 0.09375
- final_offset_entries: float32 [256], replicated, may hold values from -3 to 3
- transition: float32 [256, 256], replicated, may hold values from -1 to 1
- gains: float32 [256, 256], P('tm'), may hold values from 0 to 1
- smooth_gains: float32 [256, 256], P('tm'), may hold values from 0 to 1
Outputs:
- filtered: float32 [256, 256], P(('tm', 'mp'))
- smoothed: float32 [256, 256], P(('tm', 'mp'))
All inputs are finite; a program needn't handle non-finite values.
Results may differ from a plain program's by a relative error of at most 0.0021.
Values sent between devices are 32-bit elements; how exact they have to be, the bound alone decides.
A program may use at most 128 MiB of HBM per device.

v0:
```python
import jax
import jax.numpy as jnp
from jax import lax
from jax.sharding import PartitionSpec as P

HIGH = lax.Precision.HIGHEST


def passed_along(value, axis, steps):
    count = lax.axis_size(axis)
    initial, last = (max(0, -steps), min(count, count - steps))
    return lax.ppermute(value, axis, [(source, source + steps) for source in range(initial, last)])


def compose_diagonal(earlier, later):
    return (later[0] * earlier[0], later[0] * earlier[1] + later[1])


def sweep_up(mats, vecs):
    levels = [(mats, vecs)]
    while mats.shape[0] > 1:
        count = mats.shape[0]
        half = count // 2
        first_m = mats[0 : 2 * half : 2]
        second_m = mats[1 : 2 * half : 2]
        first_v = vecs[0 : 2 * half : 2]
        second_v = vecs[1 : 2 * half : 2]
        new_m = jnp.einsum("bij,bjk->bik", second_m, first_m, precision=HIGH)
        new_v = jnp.einsum("bij,bj->bi", second_m, first_v, precision=HIGH) + second_v
        mats, vecs = (new_m, new_v)
        levels.append((mats, vecs))
    return levels


def sweep_down(levels, incoming):
    states = incoming[None]
    for level in range(len(levels) - 2, -1, -1):
        mats, vecs = levels[level]
        count = mats.shape[0]
        half = count // 2
        evens = states
        odds = (
            jnp.einsum("bij,bj->bi", mats[0 : 2 * half : 2], evens, precision=HIGH)
            + vecs[0 : 2 * half : 2]
        )
        paired = jnp.stack([evens, odds], 1).reshape(2 * half, states.shape[1])
        states = paired
    return states


def carry_forward(block_m, block_v):
    grid = block_v.shape[0]

    def relay_time(step, incoming):
        outgoing = jnp.dot(block_m, incoming, precision=HIGH) + block_v
        return passed_along(outgoing, "tm", 1)

    return lax.fori_loop(0, lax.axis_size("tm") - 1, relay_time, jnp.zeros((grid,), jnp.float32))


def carry_backward(block_d, block_v):
    grid = block_v.shape[0]

    def relay_time(step, incoming):
        outgoing = block_d * incoming + block_v
        return passed_along(outgoing, "tm", -1)

    return lax.fori_loop(0, lax.axis_size("tm") - 1, relay_time, jnp.zeros((grid,), jnp.float32))


def on_device(
    features, w_in, b_in, output_weight, final_offset_entries, transition, gains, smooth_gains
):
    pre = jnp.dot(features, w_in, preferred_element_type=jnp.float32) + b_in
    hidden_layer = jax.nn.gelu(pre, approximate=True).astype(jnp.bfloat16)
    partial_measurement = jnp.dot(hidden_layer, output_weight, preferred_element_type=jnp.float32)
    share = features.shape[0] // lax.axis_size("mp")
    mp_place = lax.axis_index("mp")
    time_last = lax.axis_index("tm") == lax.axis_size("tm") - 1
    measured_values = lax.psum(partial_measurement, "mp") + final_offset_entries
    weight_here = smooth_gains
    forward_m = (1.0 - gains)[:, :, None] * transition[None]
    forward_variance = gains * measured_values
    levels = sweep_up(forward_m, forward_variance)
    incoming = carry_forward(levels[-1][0][0], levels[-1][1][0])
    before = sweep_down(levels, incoming)
    filtered = jnp.einsum("tij,tj->ti", forward_m, before, precision=HIGH) + forward_variance
    closing = jnp.where(time_last, 0.0, 1.0).astype(jnp.float32)
    weight_here = weight_here.at[-1].multiply(closing)
    predicted = jnp.dot(filtered, transition.T, precision=HIGH)
    backward_d = weight_here[::-1]
    backward_v = (filtered - weight_here * predicted)[::-1]
    prefix_d, prefix_v = lax.associative_scan(compose_diagonal, (backward_d, backward_v), axis=0)
    later_state = carry_backward(prefix_d[-1], prefix_v[-1])
    smoothed = (prefix_d * later_state[None] + prefix_v)[::-1]
    filtered = lax.dynamic_slice_in_dim(filtered, mp_place * share, share, 0)
    smoothed = lax.dynamic_slice_in_dim(smoothed, mp_place * share, share, 0)
    return (filtered, smoothed)


def solution(mesh):
    placed = (
        P("tm", None),
        P(None, "mp"),
        P("mp"),
        P("mp", None),
        P(),
        P(),
        P("tm", None),
        P("tm", None),
    )
    return jax.shard_map(
        on_device,
        mesh=mesh,
        in_specs=placed,
        out_specs=(P(("tm", "mp"), None), P(("tm", "mp"), None)),
        check_vma=False,
    )
```

profile of v0, /device:TPU:0, one launch (start us, length us, event | category | flops | bytes accessed | tf_op | source)
XLA Modules:
  0.0 162.2 jit_solution(11965233251702824456)
XLA Ops:
  1.7 3.2 %fusion.40 = f32[32,256]{1,0:T(8,128)S(1)} fusion(bf16[1024,256]{1,0:T(8,128)(2,1)S(1)} %copy-done, bf16[32,2048]{1,0:T(8,128)(2,1)} %param.14, bf16[2048,1024]{1,0:T(8,128)(2,1)} %param.15, f32[1024]{0:T(1024)} %param.16), kind=kOutput, calls=%fused_computation.49 | convolution fusion | flops 151322624 | bytes 4886528 | tf_op jit(solution)/shard_map/dot_general | solution.py:76
  4.9 12.9 %psum.7 = f32[32,256]{1,0:T(8,128)S(1)} all-reduce(f32[32,256]{1,0:T(8,128)S(1)} %fusion.40), channel_id=1, replica_groups=mesh['tm'=8,'mp'=4] {'mp'}, use_global_device_ids=true, to_apply=%region_0.0 | all-reduce | flops 8192 | bytes 65536 | tf_op jit(solution)/shard_map/psum | solution.py:80
  17.9 3.9 %broadcast_multiply_fusion = f32[32,256,256]{2,1,0:T(8,128)} fusion(f32[256,256]{1,0:T(8,128)S(1)} %copy-done.3, f32[32,256]{1,0:T(8,128)S(1)} %get-tuple-element.76), kind=kLoop, calls=%fused_computation.1 | loop fusion | flops 2097152 | bytes 8683520 | tf_op jit(solution)/shard_map/mul | solution.py:82
  21.8 5.8 %fusion.4 = f32[16,1,256]{2,1,0:T(1,128)S(1)} fusion(f32[32,256,256]{2,1,0:T(8,128)} %broadcast_multiply_fusion, f32[16,256,1]{1,0,2:T(8,128)S(1)} %bitcast.86), kind=kOutput, calls=%fused_computation.6 | convolution fusion | flops 12582912 | bytes 4227072 | tf_op jit(solution)/shard_map/bij,bj->bi/dot_general | solution.py:29
  27.6 8.5 %fusion.2 = f32[16,256,256]{2,1,0:T(8,128)S(1)} fusion(f32[32,256,256]{2,1,0:T(8,128)} %broadcast_multiply_fusion), kind=kOutput, calls=%fused_computation.4 | convolution fusion | flops 3221225472 | bytes 12582912 | tf_op jit(solution)/shard_map/bij,bjk->bik/dot_general | solution.py:28
  36.1 2.0 %copy-done.1 = f32[16,256,256]{2,1,0:T(8,128)} copy-done((f32[16,256,256]{2,1,0:T(8,128)}, f32[16,256,256]{2,1,0:T(8,128)S(1)}, u32[]{:S(2)}) %copy-start.1) | copy-done | bytes 4194328
  38.1 1.8 %fusion.12 = f32[8,1,256]{2,1,0:T(1,128)S(1)} fusion(f32[16,256,256]{2,1,0:T(8,128)S(1)} %fusion.2, f32[8,256,1]{1,0,2:T(8,128)S(1)} %bitcast.88), kind=kOutput, calls=%fused_computation.14 | convolution fusion | flops 6291456 | bytes 2113536 | tf_op jit(solution)/shard_map/bij,bj->bi/dot_general | solution.py:29
  40.0 4.3 %fusion.10 = f32[8,256,256]{2,1,0:T(8,128)S(1)} fusion(f32[16,256,256]{2,1,0:T(8,128)} %copy-done.1), kind=kOutput, calls=%fused_computation.12 | convolution fusion | flops 1610612736 | bytes 6291456 | tf_op jit(solution)/shard_map/bij,bjk->bik/dot_general | solution.py:28
  48.1 1.9 %fusion.26 = f32[2,256,256]{2,1,0:T(8,128)S(1)} fusion(f32[4,256,256]{2,1,0:T(8,128)} %copy-done.2), kind=kOutput, calls=%fused_computation.32 | convolution fusion | flops 402653184 | bytes 1572864 | tf_op jit(solution)/shard_map/bij,bjk->bik/dot_general | solution.py:28
  50.7 43.5 %while.21 = (s32[]{:T(128)}, f32[256]{0:T(256)S(1)}, f32[256,256]{1,0:T(8,128)S(1)}, f32[256]{0:T(256)S(1)}, s32[]{:T(128)}) while((s32[]{:T(128)}, f32[256]{0:T(256)S(1)}, f32[256,256]{1,0:T(8,128)S(1)}, f32[256]{0:T(256)S(1)}, s32[]{:T(128)}) %tuple.61), condition=%wide.region_2.0_spmd, body=%wide.region_1.0_spmd.sunk | while | flops 786690 | bytes 271461 | solution.py:58
  51.0 3.4 %collective-permute-start = (f32[256]{0:T(256)S(1)}, f32[256]{0:T(256)S(1)}, u32[]{:S(2)}, u32[]{:S(2)}) collective-permute-start(f32[256]{0:T(256)S(1)} %add.331), channel_id=1, source_target_pairs={{0,4},{4,8},{8,12},{12,16},{16,20},{20,24},{24,28},{1,5},{5,9},{9,... | collective-permute-start | bytes 3080 | tf_op jit(solution)/shard_map/while/body/eval_jaxpr/ppermute | solution.py:12
  56.0 4.2 %collective-permute-start = (f32[256]{0:T(256)S(1)}, f32[256]{0:T(256)S(1)}, u32[]{:S(2)}, u32[]{:S(2)}) collective-permute-start(f32[256]{0:T(256)S(1)} %add.331), channel_id=1, source_target_pairs={{0,4},{4,8},{8,12},{12,16},{16,20},{20,24},{24,28},{1,5},{5,9},{9,... | collective-permute-start | bytes 3080 | tf_op jit(solution)/shard_map/while/body/eval_jaxpr/ppermute | solution.py:12
  61.8 4.4 %collective-permute-start = (f32[256]{0:T(256)S(1)}, f32[256]{0:T(256)S(1)}, u32[]{:S(2)}, u32[]{:S(2)}) collective-permute-start(f32[256]{0:T(256)S(1)} %add.331), channel_id=1, source_target_pairs={{0,4},{4,8},{8,12},{12,16},{16,20},{20,24},{24,28},{1,5},{5,9},{9,... | collective-permute-start | bytes 3080 | tf_op jit(solution)/shard_map/while/body/eval_jaxpr/ppermute | solution.py:12
  67.7 5.1 %collective-permute-start = (f32[256]{0:T(256)S(1)}, f32[256]{0:T(256)S(1)}, u32[]{:S(2)}, u32[]{:S(2)}) collective-permute-start(f32[256]{0:T(256)S(1)} %add.331), channel_id=1, source_target_pairs={{0,4},{4,8},{8,12},{12,16},{16,20},{20,24},{24,28},{1,5},{5,9},{9,... | collective-permute-start | bytes 3080 | tf_op jit(solution)/shard_map/while/body/eval_jaxpr/ppermute | solution.py:12
  74.4 5.1 %collective-permute-start = (f32[256]{0:T(256)S(1)}, f32[256]{0:T(256)S(1)}, u32[]{:S(2)}, u32[]{:S(2)}) collective-permute-start(f32[256]{0:T(256)S(1)} %add.331), channel_id=1, source_target_pairs={{0,4},{4,8},{8,12},{12,16},{16,20},{20,24},{24,28},{1,5},{5,9},{9,... | collective-permute-start | bytes 3080 | tf_op jit(solution)/shard_map/while/body/eval_jaxpr/ppermute | solution.py:12
  81.1 5.1 %collective-permute-start = (f32[256]{0:T(256)S(1)}, f32[256]{0:T(256)S(1)}, u32[]{:S(2)}, u32[]{:S(2)}) collective-permute-start(f32[256]{0:T(256)S(1)} %add.331), channel_id=1, source_target_pairs={{0,4},{4,8},{8,12},{12,16},{16,20},{20,24},{24,28},{1,5},{5,9},{9,... | collective-permute-start | bytes 3080 | tf_op jit(solution)/shard_map/while/body/eval_jaxpr/ppermute | solution.py:12
  87.8 5.1 %collective-permute-start = (f32[256]{0:T(256)S(1)}, f32[256]{0:T(256)S(1)}, u32[]{:S(2)}, u32[]{:S(2)}) collective-permute-start(f32[256]{0:T(256)S(1)} %add.331), channel_id=1, source_target_pairs={{0,4},{4,8},{8,12},{12,16},{16,20},{20,24},{24,28},{1,5},{5,9},{9,... | collective-permute-start | bytes 3080 | tf_op jit(solution)/shard_map/while/body/eval_jaxpr/ppermute | solution.py:12
  94.6 1.6 %fusion.24 = f32[2,1,256]{2,1,0:T(1,128)S(1)} fusion(f32[4,256,256]{2,1,0:T(8,128)} %copy-done.2, f32[2,256,1]{1,0,2:T(2,128)S(1)} %get-tuple-element.101), kind=kOutput, calls=%fused_computation.30 | convolution fusion | flops 1572864 | bytes 528384 | tf_op jit(solution)/shard_map/bij,bj->bi/dot_general | solution.py:43
  97.3 3.4 %fusion.8 = f32[8,1,256]{2,1,0:T(1,128)S(1)} fusion(f32[8,256,1]{1,2,0:T(1,128)S(1)} %reshape.98, f32[16,256,256]{2,1,0:T(8,128)} %copy-done.1), kind=kOutput, calls=%fused_computation.10 | convolution fusion | flops 6291456 | bytes 2113536 | tf_op jit(solution)/shard_map/bij,bj->bi/dot_general | solution.py:43
  100.9 5.8 %fusion = f32[16,1,256]{2,1,0:T(1,128)S(1)} fusion(f32[16,256,1]{1,2,0:T(1,128)S(1)} %reshape.100, f32[32,256,256]{2,1,0:T(8,128)} %broadcast_multiply_fusion), kind=kOutput, calls=%fused_computation.2 | convolution fusion | flops 12582912 | bytes 4227072 | tf_op jit(solution)/shard_map/bij,bj->bi/dot_general | solution.py:43
  106.8 7.6 %fusion.7 = f32[32,1,256]{2,1,0:T(1,128)S(1)} fusion(f32[32,256,1]{1,2,0:T(1,128)S(1)} %reshape.102, f32[256,256]{1,0:T(8,128)S(1)} %copy-done.4, f32[32,256]{1,0:T(8,128)S(1)} %get-tuple-element.76), kind=kOutput, calls=%fused_computation.9 | convolution fusion | flops 27262976 | bytes 360448 | tf_op jit(solution)/shard_map/tij,tj->ti/dot_general | solution.py:87
  116.4 45.1 %while.22 = (s32[]{:T(128)}, f32[256]{0:T(256)S(1)}, f32[256]{0:T(256)S(1)}, f32[256]{0:T(256)S(1)}, s32[]{:T(128)}) while((s32[]{:T(128)}, f32[256]{0:T(256)S(1)}, f32[256]{0:T(256)S(1)}, f32[256]{0:T(256)S(1)}, s32[]{:T(128)}) %tuple.63), condition=%wide.region_4.5_spmd, body=%wide.region_3.4_spmd.sunk | while | flops 514 | bytes 8293 | solution.py:68
  116.4 1.3 collective-permute-start.1
  117.7 5.3 %collective-permute-done.1 = f32[256]{0:T(256)S(1)} collective-permute-done((f32[256]{0:T(256)S(1)}, f32[256]{0:T(256)S(1)}, u32[]{:S(2)}, u32[]{:S(2)}) %collective-permute-start.1) | collective-permute-done | bytes 1056 | tf_op jit(solution)/shard_map/while/body/eval_jaxpr/ppermute | solution.py:12
  123.0 1.3 collective-permute-start.1
  124.3 5.3 %collective-permute-done.1 = f32[256]{0:T(256)S(1)} collective-permute-done((f32[256]{0:T(256)S(1)}, f32[256]{0:T(256)S(1)}, u32[]{:S(2)}, u32[]{:S(2)}) %collective-permute-start.1) | collective-permute-done | bytes 1056 | tf_op jit(solution)/shard_map/while/body/eval_jaxpr/ppermute | solution.py:12
  131.0 5.1 %collective-permute-done.1 = f32[256]{0:T(256)S(1)} collective-permute-done((f32[256]{0:T(256)S(1)}, f32[256]{0:T(256)S(1)}, u32[]{:S(2)}, u32[]{:S(2)}) %collective-permute-start.1) | collective-permute-done | bytes 1056 | tf_op jit(solution)/shard_map/while/body/eval_jaxpr/ppermute | solution.py:12
  137.3 5.1 %collective-permute-done.1 = f32[256]{0:T(256)S(1)} collective-permute-done((f32[256]{0:T(256)S(1)}, f32[256]{0:T(256)S(1)}, u32[]{:S(2)}, u32[]{:S(2)}) %collective-permute-start.1) | collective-permute-done | bytes 1056 | tf_op jit(solution)/shard_map/while/body/eval_jaxpr/ppermute | solution.py:12
  142.4 1.3 collective-permute-start.1
  143.7 5.1 %collective-permute-done.1 = f32[256]{0:T(256)S(1)} collective-permute-done((f32[256]{0:T(256)S(1)}, f32[256]{0:T(256)S(1)}, u32[]{:S(2)}, u32[]{:S(2)}) %collective-permute-start.1) | collective-permute-done | bytes 1056 | tf_op jit(solution)/shard_map/while/body/eval_jaxpr/ppermute | solution.py:12
  150.0 5.1 %collective-permute-done.1 = f32[256]{0:T(256)S(1)} collective-permute-done((f32[256]{0:T(256)S(1)}, f32[256]{0:T(256)S(1)}, u32[]{:S(2)}, u32[]{:S(2)}) %collective-permute-start.1) | collective-permute-done | bytes 1056 | tf_op jit(solution)/shard_map/while/body/eval_jaxpr/ppermute | solution.py:12
  156.4 5.1 %collective-permute-done.1 = f32[256]{0:T(256)S(1)} collective-permute-done((f32[256]{0:T(256)S(1)}, f32[256]{0:T(256)S(1)}, u32[]{:S(2)}, u32[]{:S(2)}) %collective-permute-start.1) | collective-permute-done | bytes 1056 | tf_op jit(solution)/shard_map/while/body/eval_jaxpr/ppermute | solution.py:12
  (171 shorter events, 25.5 us)
Async XLA Ops:
  0.6 1.1 copy-start
  0.6 17.2 %copy-start.6 = (f32[256]{0:T(256)S(1)}, f32[256]{0:T(256)}, u32[]{:S(2)}) copy-start(f32[256]{0:T(256)} %param.18) | copy-start | bytes 3076
  0.7 17.2 %copy-start.5 = (f32[32,256]{1,0:T(8,128)S(1)}, f32[32,256]{1,0:T(8,128)}, u32[]{:S(2)}) copy-start(f32[32,256]{1,0:T(8,128)} %param.20) | copy-start | bytes 98308
  0.7 17.2 %copy-start.3 = (f32[256,256]{1,0:T(8,128)S(1)}, f32[256,256]{1,0:T(8,128)}, u32[]{:S(2)}) copy-start(f32[256,256]{1,0:T(8,128)} %param.19) | copy-start | bytes 786436
  36.1 2.0 %copy-start.1 = (f32[16,256,256]{2,1,0:T(8,128)}, f32[16,256,256]{2,1,0:T(8,128)S(1)}, u32[]{:S(2)}) copy-start(f32[16,256,256]{2,1,0:T(8,128)S(1)} %fusion.2) | copy-start | bytes 12582916
  46.5 1.0 copy-start.2
  51.0 4.7 %collective-permute-start = (f32[256]{0:T(256)S(1)}, f32[256]{0:T(256)S(1)}, u32[]{:S(2)}, u32[]{:S(2)}) collective-permute-start(f32[256]{0:T(256)S(1)} %add.331), channel_id=1, source_target_pairs={{0,4},{4,8},{8,12},{12,16},{16,20},{20,24},{24,28},{1,5},{5,9},{9,... | collective-permute-start | bytes 3080 | tf_op jit(solution)/shard_map/while/body/eval_jaxpr/ppermute | solution.py:12
  56.0 5.5 %collective-permute-start = (f32[256]{0:T(256)S(1)}, f32[256]{0:T(256)S(1)}, u32[]{:S(2)}, u32[]{:S(2)}) collective-permute-start(f32[256]{0:T(256)S(1)} %add.331), channel_id=1, source_target_pairs={{0,4},{4,8},{8,12},{12,16},{16,20},{20,24},{24,28},{1,5},{5,9},{9,... | collective-permute-start | bytes 3080 | tf_op jit(solution)/shard_map/while/body/eval_jaxpr/ppermute | solution.py:12
  61.8 5.7 %collective-permute-start = (f32[256]{0:T(256)S(1)}, f32[256]{0:T(256)S(1)}, u32[]{:S(2)}, u32[]{:S(2)}) collective-permute-start(f32[256]{0:T(256)S(1)} %add.331), channel_id=1, source_target_pairs={{0,4},{4,8},{8,12},{12,16},{16,20},{20,24},{24,28},{1,5},{5,9},{9,... | collective-permute-start | bytes 3080 | tf_op jit(solution)/shard_map/while/body/eval_jaxpr/ppermute | solution.py:12
  67.7 6.4 %collective-permute-start = (f32[256]{0:T(256)S(1)}, f32[256]{0:T(256)S(1)}, u32[]{:S(2)}, u32[]{:S(2)}) collective-permute-start(f32[256]{0:T(256)S(1)} %add.331), channel_id=1, source_target_pairs={{0,4},{4,8},{8,12},{12,16},{16,20},{20,24},{24,28},{1,5},{5,9},{9,... | collective-permute-start | bytes 3080 | tf_op jit(solution)/shard_map/while/body/eval_jaxpr/ppermute | solution.py:12
  74.4 6.4 %collective-permute-start = (f32[256]{0:T(256)S(1)}, f32[256]{0:T(256)S(1)}, u32[]{:S(2)}, u32[]{:S(2)}) collective-permute-start(f32[256]{0:T(256)S(1)} %add.331), channel_id=1, source_target_pairs={{0,4},{4,8},{8,12},{12,16},{16,20},{20,24},{24,28},{1,5},{5,9},{9,... | collective-permute-start | bytes 3080 | tf_op jit(solution)/shard_map/while/body/eval_jaxpr/ppermute | solution.py:12
  81.1 6.4 %collective-permute-start = (f32[256]{0:T(256)S(1)}, f32[256]{0:T(256)S(1)}, u32[]{:S(2)}, u32[]{:S(2)}) collective-permute-start(f32[256]{0:T(256)S(1)} %add.331), channel_id=1, source_target_pairs={{0,4},{4,8},{8,12},{12,16},{16,20},{20,24},{24,28},{1,5},{5,9},{9,... | collective-permute-start | bytes 3080 | tf_op jit(solution)/shard_map/while/body/eval_jaxpr/ppermute | solution.py:12
  87.8 6.4 %collective-permute-start = (f32[256]{0:T(256)S(1)}, f32[256]{0:T(256)S(1)}, u32[]{:S(2)}, u32[]{:S(2)}) collective-permute-start(f32[256]{0:T(256)S(1)} %add.331), channel_id=1, source_target_pairs={{0,4},{4,8},{8,12},{12,16},{16,20},{20,24},{24,28},{1,5},{5,9},{9,... | collective-permute-start | bytes 3080 | tf_op jit(solution)/shard_map/while/body/eval_jaxpr/ppermute | solution.py:12
  94.6 12.2 %copy-start.4 = (f32[256,256]{1,0:T(8,128)S(1)}, f32[256,256]{1,0:T(8,128)}, u32[]{:S(2)}) copy-start(f32[256,256]{1,0:T(8,128)} %param.19) | copy-start | bytes 786436
  116.4 6.6 %collective-permute-start.1 = (f32[256]{0:T(256)S(1)}, f32[256]{0:T(256)S(1)}, u32[]{:S(2)}, u32[]{:S(2)}) collective-permute-start(f32[256]{0:T(256)S(1)} %multiply_add_fusion.7), channel_id=1, source_target_pairs={{4,0},{8,4},{12,8},{16,12},{20,16},{24,20},{28,24},{5,1},{9,5},{13... | collective-permute-start | bytes 3080 | tf_op jit(solution)/shard_map/while/body/eval_jaxpr/ppermute | solution.py:12
  123.0 6.6 %collective-permute-start.1 = (f32[256]{0:T(256)S(1)}, f32[256]{0:T(256)S(1)}, u32[]{:S(2)}, u32[]{:S(2)}) collective-permute-start(f32[256]{0:T(256)S(1)} %multiply_add_fusion.7), channel_id=1, source_target_pairs={{4,0},{8,4},{12,8},{16,12},{20,16},{24,20},{28,24},{5,1},{9,5},{13... | collective-permute-start | bytes 3080 | tf_op jit(solution)/shard_map/while/body/eval_jaxpr/ppermute | solution.py:12
  129.7 6.4 %collective-permute-start.1 = (f32[256]{0:T(256)S(1)}, f32[256]{0:T(256)S(1)}, u32[]{:S(2)}, u32[]{:S(2)}) collective-permute-start(f32[256]{0:T(256)S(1)} %multiply_add_fusion.7), channel_id=1, source_target_pairs={{4,0},{8,4},{12,8},{16,12},{20,16},{24,20},{28,24},{5,1},{9,5},{13... | collective-permute-start | bytes 3080 | tf_op jit(solution)/shard_map/while/body/eval_jaxpr/ppermute | solution.py:12
  136.0 6.4 %collective-permute-start.1 = (f32[256]{0:T(256)S(1)}, f32[256]{0:T(256)S(1)}, u32[]{:S(2)}, u32[]{:S(2)}) collective-permute-start(f32[256]{0:T(256)S(1)} %multiply_add_fusion.7), channel_id=1, source_target_pairs={{4,0},{8,4},{12,8},{16,12},{20,16},{24,20},{28,24},{5,1},{9,5},{13... | collective-permute-start | bytes 3080 | tf_op jit(solution)/shard_map/while/body/eval_jaxpr/ppermute | solution.py:12
  142.4 6.4 %collective-permute-start.1 = (f32[256]{0:T(256)S(1)}, f32[256]{0:T(256)S(1)}, u32[]{:S(2)}, u32[]{:S(2)}) collective-permute-start(f32[256]{0:T(256)S(1)} %multiply_add_fusion.7), channel_id=1, source_target_pairs={{4,0},{8,4},{12,8},{16,12},{20,16},{24,20},{28,24},{5,1},{9,5},{13... | collective-permute-start | bytes 3080 | tf_op jit(solution)/shard_map/while/body/eval_jaxpr/ppermute | solution.py:12
  148.7 6.4 %collective-permute-start.1 = (f32[256]{0:T(256)S(1)}, f32[256]{0:T(256)S(1)}, u32[]{:S(2)}, u32[]{:S(2)}) collective-permute-start(f32[256]{0:T(256)S(1)} %multiply_add_fusion.7), channel_id=1, source_target_pairs={{4,0},{8,4},{12,8},{16,12},{20,16},{24,20},{28,24},{5,1},{9,5},{13... | collective-permute-start | bytes 3080 | tf_op jit(solution)/shard_map/while/body/eval_jaxpr/ppermute | solution.py:12
  155.1 6.4 %collective-permute-start.1 = (f32[256]{0:T(256)S(1)}, f32[256]{0:T(256)S(1)}, u32[]{:S(2)}, u32[]{:S(2)}) collective-permute-start(f32[256]{0:T(256)S(1)} %multiply_add_fusion.7), channel_id=1, source_target_pairs={{4,0},{8,4},{12,8},{16,12},{20,16},{24,20},{28,24},{5,1},{9,5},{13... | collective-permute-start | bytes 3080 | tf_op jit(solution)/shard_map/while/body/eval_jaxpr/ppermute | solution.py:12
where the time goes:
time: 163 us; the launch traced here: 162 us
  matrix products  50.8 us (31%)
  waiting for transfers between devices  44.9 us (28%)
  starting transfers between devices  41.5 us (25%)
  blocking collectives  12.9 us (8%)
  local copies, waits for them, and re-layouts  6.12 us (4%)
  other arithmetic  4.38 us (3%)
    ppermute x14, waiting for transfers between devices, passed_along(): lax.ppermute(value, axis, [(source, source + steps) for source in range(i...  44.9 us
    ppermute x14, starting transfers between devices, passed_along(): lax.ppermute(value, axis, [(source, source + steps) for source in range(i...  41.5 us
    dot_general x5, matrix products, sweep_up(): new_m = jnp.einsum('bij,bjk->bik', second_m, first_m, precision=HIGH)  16.2 us
    psum x1, blocking collectives, on_device(): measured_values = lax.psum(partial_measurement, 'mp') + final_offset_entries  12.9 us
    dot_general x5, matrix products, sweep_down(): jnp.einsum('bij,bj->bi', mats[0:2 * half:2], evens, precision=HIGH)  12.1 us
    dot_general x5, matrix products, sweep_up(): jnp.einsum('bij,bj->bi', second_m, first_v, precision=HIGH) + second_v  9.4 us
    dot_general x1, matrix products, on_device(): jnp.einsum('tij,tj->ti', forward_m, before, precision=HIGH)  7.61 us
    unnamed x15, local copies, waits for them, and re-layouts  4.02 us
  transfers between devices with their start and end apart: 14, of which 14 were waited for; matrix products, arithmetic and copies ran while one was open for 0% of the time, Pallas kernels for 0%

commit v1 on v0

v1 whole, which is shorter than its diff:
```python
import functools

import jax
import jax.numpy as jnp
from jax import lax
from jax.experimental import pallas as pl
from jax.experimental.pallas import tpu as pltpu
from jax.sharding import PartitionSpec as P

MESH = pl.DeviceIdType.MESH
F32 = jnp.float32
BF16 = jnp.bfloat16


def split(value):
    high = value.astype(BF16).astype(F32)
    return high, value - high


def store_split(target, value):
    width = value.shape[1]
    high, rest = split(value)
    target[:, :width] = high.astype(BF16)
    target[:, width:] = rest.astype(BF16)


def times(rows, pair):
    count, width = rows.shape
    both = jnp.concatenate(split(rows), 0).astype(BF16)
    out = jnp.dot(both, pair[...], preferred_element_type=F32)
    return out[:count, :width] + out[count:, :width] + out[:count, width:]


def kernel(
    tm, mp, chunks,
    feat_h, w_in_h, b_h, w2_h, off_h, trans_h, gains_h, sg_h,
    filt_o, smooth_o,
    feat, w_in, b_v, w2, off, trans, gains, sg,
    at, at_pair, m_pair, phi_pair, part, meas, snap, m_all, phi_all, vel, x_in, x_out, x_own,
    f8, u8, e8, comp, comps,
    in_sem, part_ss, part_rs, m_ss, m_rs, phi_ss, phi_rs, chain_ss, chain_rs, back_ss, back_rs,
):
    c, k = lax.axis_index("tm"), lax.axis_index("mp")
    place = c * mp + k
    total = tm * mp
    frames, grid = gains.shape
    share = frames // mp
    quarter = grid // mp
    depth = feat.shape[1] // chunks

    def fetch(source, target, slot):
        copy = pltpu.make_async_copy(source, target, in_sem.at[slot])
        copy.start()
        return copy

    get_trans = fetch(trans_h, trans, 0)
    get_gains = fetch(gains_h, gains, 1)
    get_feat = fetch(feat_h, feat, 2)
    get_w = [
        fetch(w_in_h.at[pl.ds(r * depth, depth), :], w_in.at[pl.ds(r * depth, depth), :], 8 + r)
        for r in range(chunks)
    ]
    get_b = fetch(b_h, b_v, 3)
    get_w2 = fetch(w2_h, w2, 4)
    get_off = fetch(off_h, off, 5)
    get_sg = fetch(sg_h, sg, 6)

    barrier = pltpu.get_barrier_semaphore()

    def greet(step, carry):
        other = lax.rem(place + step, total)
        pl.semaphore_signal(
            barrier, inc=1, device_id={"tm": other // mp, "mp": lax.rem(other, mp)},
            device_id_type=MESH,
        )
        return carry

    lax.fori_loop(1, total, greet, 0)

    get_trans.wait()
    get_gains.wait()
    at[...] = jnp.transpose(trans[...])
    store_split(at_pair, at[...])
    rows = at[pl.ds(pl.multiple_of(k * quarter, quarter), quarter), :] * (1.0 - gains[0:1, :])
    get_feat.wait()
    pre = jnp.zeros((frames, w_in.shape[1]), F32)
    pace = frames // chunks
    for r in range(chunks):
        get_w[r].wait()
        pre += jnp.dot(
            feat[:, r * depth : (r + 1) * depth], w_in[r * depth : (r + 1) * depth, :],
            preferred_element_type=F32,
        )
        for t in range(r * pace, (r + 1) * pace):
            if t > 0:
                rows = times(rows, at_pair) * (1.0 - gains[t : t + 1, :])
            if (t + 1) % share == 0:
                snap[(t + 1) // share - 1] = rows
    get_b.wait()
    get_w2.wait()
    hidden = jax.nn.gelu(pre + b_v[...], approximate=True).astype(BF16)
    part[k] = jnp.dot(hidden, w2[...], preferred_element_type=F32)

    pl.semaphore_wait(barrier, total - 1)

    def to_peer(step, source, target, send, recv):
        peer = lax.rem(k + step, mp)
        return pltpu.make_async_remote_copy(
            source, target, send.at[step], recv.at[step],
            device_id={"tm": c, "mp": peer}, device_id_type=MESH,
        )

    def phi_copy(step):
        peer = lax.rem(k + step, mp)
        return pltpu.make_async_remote_copy(
            snap.at[lax.rem(peer + mp - 1, mp)], phi_all.at[k], phi_ss.at[step], phi_rs.at[step],
            device_id={"tm": c, "mp": peer}, device_id_type=MESH,
        )

    part_copies = [to_peer(s, part.at[k], part.at[k], part_ss, part_rs) for s in range(1, mp)]
    m_copies = [to_peer(s, snap.at[mp - 1], m_all.at[k], m_ss, m_rs) for s in range(1, mp)]
    phi_copies = [phi_copy(s) for s in range(1, mp)]
    for copy in part_copies:
        copy.start()
    for copy in m_copies:
        copy.start()
    for copy in phi_copies:
        copy.start()
    m_all[k] = snap[mp - 1]
    phi_all[k] = snap[lax.rem(k + mp - 1, mp)]
    get_off.wait()
    get_sg.wait()
    for copy in part_copies:
        copy.wait_recv()
    measured = off[...]
    for peer in range(mp):
        measured = measured + part[peer]
    meas[...] = gains[...] * measured

    def frame(t, state):
        keep = 1.0 - gains[pl.ds(t, 1), :]
        return times(state, at_pair) * keep + meas[pl.ds(t, 1), :]

    def pass_frames(block, state):
        for j in range(share):
            t = block * share + j
            state = frame(t, state)
            vel[pl.ds(t, 1), :] = state[0:1]
        return state

    vel_end = lax.fori_loop(0, mp, pass_frames, jnp.zeros((8, grid), F32))
    for copy in m_copies:
        copy.wait_recv()
    store_split(m_pair, m_all[...].reshape(grid, grid))
    for copy in phi_copies:
        copy.wait_recv()
    store_split(phi_pair, phi_all[...].reshape(grid, grid))

    chain = pltpu.make_async_remote_copy(
        x_out, x_in, chain_ss, chain_rs,
        device_id={"tm": lax.rem(c + 1, tm), "mp": k}, device_id_type=MESH,
    )

    @pl.when(c == 0)
    def _():
        x_in[...] = jnp.zeros_like(x_in)
        x_out[...] = vel_end

    @pl.when(c > 0)
    def _():
        chain.wait_recv()
        x_out[...] = times(x_in[...], m_pair) + vel_end

    @pl.when(c < tm - 1)
    def _():
        chain.start()

    @pl.when(k == 0)
    def _():
        x_own[...] = x_in[...]

    @pl.when(k > 0)
    def _():
        x_own[...] = times(x_in[...], phi_pair) + vel[pl.ds(k * share - 1, 1), :]

    state = x_own[...]
    for j in range(share):
        state = frame(k * share + j, state)
        f8[j : j + 1, :] = state[0:1]
    filtered = f8[...]
    filt_o[...] = filtered
    last = jnp.where(place == total - 1, 0.0, 1.0).astype(F32)
    row = lax.broadcasted_iota(jnp.int32, (share, grid), 0)
    weight = sg[pl.ds(pl.multiple_of(k * share, share), share), :]
    weight = jnp.where(row == share - 1, weight * last, weight)
    e8[...] = weight
    u8[...] = filtered - weight * times(filtered, at_pair)
    slope = jnp.ones((1, grid), F32)
    value = jnp.zeros((1, grid), F32)
    for j in range(share - 1, -1, -1):
        slope = slope * e8[j : j + 1, :]
        value = u8[j : j + 1, :] + e8[j : j + 1, :] * value
    comp[0:1, :] = slope
    comp[1:2, :] = value

    def back_copy(other):
        return pltpu.make_async_remote_copy(
            comp, comps.at[place], back_ss.at[other], back_rs.at[place],
            device_id={"tm": other // mp, "mp": lax.rem(other, mp)}, device_id_type=MESH,
        )

    def send_back(step, carry):
        back_copy(place - 1 - step).start()
        return carry

    lax.fori_loop(0, place, send_back, 0)

    def gather_back(step, later):
        source = total - 1 - step
        pltpu.make_async_remote_copy(
            comp, comps.at[source], back_ss.at[source], back_rs.at[source],
            device_id={"tm": source // mp, "mp": lax.rem(source, mp)}, device_id_type=MESH,
        ).wait_recv()
        both = comps[source]
        return both[0:1] * later + both[1:2]

    later = lax.fori_loop(0, total - 1 - place, gather_back, jnp.zeros((1, grid), F32))
    for j in range(share - 1, -1, -1):
        later = u8[j : j + 1, :] + e8[j : j + 1, :] * later
        smooth_o[j : j + 1, :] = later

    def end_back(other, carry):
        back_copy(other).wait_send()
        return carry

    lax.fori_loop(0, place, end_back, 0)
    for copy in part_copies + m_copies + phi_copies:
        copy.wait_send()

    @pl.when(c < tm - 1)
    def _():
        chain.wait_send()


def on_device(features, w_in, b_in, output_weight, offset, transition, gains, smooth_gains):
    tm, mp = lax.axis_size("tm"), lax.axis_size("mp")
    frames, lags = features.shape
    units = w_in.shape[1]
    grid = transition.shape[0]
    share = frames // mp
    quarter = grid // mp
    chunks = 8
    args = (
        features, w_in, b_in.reshape(1, units), output_weight, offset.reshape(1, grid),
        transition, gains, smooth_gains,
    )
    dma = pltpu.SemaphoreType.DMA
    out = jax.ShapeDtypeStruct((share, grid), F32)
    return pl.pallas_call(
        functools.partial(kernel, tm, mp, chunks),
        out_shape=(out, out),
        in_specs=[pl.BlockSpec(memory_space=pl.ANY)] * len(args),
        out_specs=(pl.BlockSpec(memory_space=pltpu.VMEM),) * 2,
        scratch_shapes=[pltpu.VMEM(a.shape, a.dtype) for a in args]
        + [
            pltpu.VMEM((grid, grid), F32),
            pltpu.VMEM((grid, 2 * grid), BF16),
            pltpu.VMEM((grid, 2 * grid), BF16),
            pltpu.VMEM((grid, 2 * grid), BF16),
            pltpu.VMEM((mp, frames, grid), F32),
            pltpu.VMEM((frames, grid), F32),
            pltpu.VMEM((mp, quarter, grid), F32),
            pltpu.VMEM((mp, quarter, grid), F32),
            pltpu.VMEM((mp, quarter, grid), F32),
            pltpu.VMEM((frames, grid), F32),
            pltpu.VMEM((8, grid), F32),
            pltpu.VMEM((8, grid), F32),
            pltpu.VMEM((8, grid), F32),
            pltpu.VMEM((share, grid), F32),
            pltpu.VMEM((share, grid), F32),
            pltpu.VMEM((share, grid), F32),
            pltpu.VMEM((2, grid), F32),
            pltpu.VMEM((tm * mp, 2, grid), F32),
            dma((8 + chunks,)),
            dma((mp,)), dma((mp,)), dma((mp,)), dma((mp,)), dma((mp,)), dma((mp,)),
            dma(()), dma(()),
            dma((tm * mp,)), dma((tm * mp,)),
        ],
        compiler_params=pltpu.CompilerParams(collective_id=0, has_side_effects=True),
        name="track",
    )(*args)


def solution(mesh):
    placed = (
        P("tm", None),
        P(None, "mp"),
        P("mp"),
        P("mp", None),
        P(),
        P(),
        P("tm", None),
        P("tm", None),
    )
    return jax.shard_map(
        on_device,
        mesh=mesh,
        in_specs=placed,
        out_specs=(P(("tm", "mp"), None), P(("tm", "mp"), None)),
        check_vma=False,
    )
```

time: 163 us -> 49 us (0.30)
  matrix products: 50.8 us -> 0 us
  Pallas kernels: 0 us -> 45.5 us
  waiting for transfers between devices: 44.9 us -> 0 us
  starting transfers between devices: 41.5 us -> 0 us
  blocking collectives: 12.9 us -> 0 us
  other arithmetic: 4.38 us -> 0 us
  local copies, waits for them, and re-layouts: 6.12 us -> 2.59 us
    dot_general x25 -> x0, matrix products: 50.8 us -> none  [the longest x5 16.2 us: sweep_up(): new_m = jnp.einsum('bij,bjk->bik', second_m, first_m, precision=HIGH)]
    pallas_call x0 -> x1, Pallas kernels: none -> 45.5 us  [on_device(): pl.pallas_call(functools.partial(kernel, tm, mp, chunks), out_shape=(out,...]
    ppermute x14 -> x0, waiting for transfers between devices: 44.9 us -> none  [passed_along(): lax.ppermute(value, axis, [(source, source + steps) for source in range(i...]
    ppermute x14 -> x0, starting transfers between devices: 41.5 us -> none  [passed_along(): lax.ppermute(value, axis, [(source, source + steps) for source in range(i...]
    psum x1 -> x0, blocking collectives: 12.9 us -> none  [on_device(): measured_values = lax.psum(partial_measurement, 'mp') + final_offset_entries]
    mul x10 -> x0, other arithmetic: 3.98 us -> none  [the longest x1 3.91 us: on_device(): forward_m = (1.0 - gains)[:, :, None] * transition[None]]
    unnamed x15 -> x2, local copies, waits for them, and re-layouts: 4.02 us -> 2.59 us
  transfers between devices with their start and end apart: 14 -> 0, of which waited for: 14 -> 0; matrix products, arithmetic and copies ran while one was open for 0% -> 0% of each run, Pallas kernels for 0% -> 0%
where the time goes in v1:
time: 49 us; the launch traced here: 48.7 us
  Pallas kernels  45.5 us (93%)
  local copies, waits for them, and re-layouts  2.59 us (5%)
  between operations  0.64 us (1%)
    pallas_call x1, Pallas kernels, on_device(): pl.pallas_call(functools.partial(kernel, tm, mp, chunks), out_shape=(out,...  45.5 us
    unnamed x2, local copies, waits for them, and re-layouts  2.59 us

profile of v1, /device:TPU:0, one launch (start us, length us, event | category | flops | bytes accessed | tf_op | source)
XLA Modules:
  0.0 48.7 jit_solution(5729658645576262057)
XLA Ops:
  0.6 45.5 %track.1 = (f32[8,256]{1,0:T(8,128)}, f32[8,256]{1,0:T(8,128)}) custom-call(bf16[32,2048]{1,0:T(8,128)(2,1)} %feat_h.1, bf16[2048,1024]{1,0:T(8,128)(2,1)} %w_in_h.1, f32[1,1024]{1,0:T(1,128)} %bitcast.2, bf16[1024,256]{1,0:T(8,128)(2,1)} %w2_h.1, f32[1,256]{1,0:T(1,128)} %bitcast.3, f32[256,256]{1,0:T(8,128)} %trans_h.1, f32[32,256]{1,0:T(8,128)} %gains_h.1, ...), custom_call_target="tpu_custom_call" | custom-call | tf_op jit(solution)/shard_map/track/pallas_call | solution.py:259
  46.1 1.3 %copy.12 = f32[8,256]{1,0:T(8,128)} copy(f32[8,256]{1,0:T(8,128)} %get-tuple-element.4) | data formatting | bytes 16384
  47.4 1.3 %copy.13 = f32[8,256]{1,0:T(8,128)} copy(f32[8,256]{1,0:T(8,128)} %get-tuple-element.5) | data formatting | bytes 16384

commit v2 on v1

--- a/solution.py
+++ b/solution.py
@@ -1,4 +1,5 @@
 import functools
+import math
 
 import jax
 import jax.numpy as jnp
@@ -10,6 +11,7 @@
 MESH = pl.DeviceIdType.MESH
 F32 = jnp.float32
 BF16 = jnp.bfloat16
+GROUP = 4
 
 
 def split(value):
@@ -32,17 +34,22 @@
 
 
 def kernel(
-    tm, mp, chunks,
+    tm, mp, chunks, group,
     feat_h, w_in_h, b_h, w2_h, off_h, trans_h, gains_h, sg_h,
-    filt_o, smooth_o,
+    packed,
     feat, w_in, b_v, w2, off, trans, gains, sg,
-    at, at_pair, m_pair, phi_pair, part, meas, snap, m_all, phi_all, vel, x_in, x_out, x_own,
+    at, at_pair, m_pair, phi_pair, part, meas, snap, m_all, phi_all, vel, v_all, x_in, x_out, x_own,
     f8, u8, e8, comp, comps,
-    in_sem, part_ss, part_rs, m_ss, m_rs, phi_ss, phi_rs, chain_ss, chain_rs, back_ss, back_rs,
+    in_sem, part_ss, part_rs, r1_ss, r1_rs, r2_ss, r2_rs, r3_ss, r3_rs, r4_ss, r4_rs,
+    phi_ss, phi_rs, v_ss, v_rs, chain_ss, chain_rs, back_ss, back_rs,
 ):
     c, k = lax.axis_index("tm"), lax.axis_index("mp")
     place = c * mp + k
     total = tm * mp
+    here, set_c = lax.rem(c, group), c // group
+    sets = tm // group
+    across = lax.rem(k + mp // 2, mp)
+    beside = k + 1 - 2 * lax.rem(k, 2)
     frames, grid = gains.shape
     share = frames // mp
     quarter = grid // mp
@@ -84,18 +91,22 @@
     rows = at[pl.ds(pl.multiple_of(k * quarter, quarter), quarter), :] * (1.0 - gains[0:1, :])
     get_feat.wait()
     pre = jnp.zeros((frames, w_in.shape[1]), F32)
-    pace = frames // chunks
+    def advance(rows, first, end):
+        for t in range(first, end):
+            if t > 0:
+                rows = times(rows, at_pair) * (1.0 - gains[t : t + 1, :])
+            if (t + 1) % share == 0:
+                snap[(t + 1) // share - 1] = rows
+        return rows
+
+    pace = frames // chunks // 2
     for r in range(chunks):
         get_w[r].wait()
         pre += jnp.dot(
             feat[:, r * depth : (r + 1) * depth], w_in[r * depth : (r + 1) * depth, :],
             preferred_element_type=F32,
         )
-        for t in range(r * pace, (r + 1) * pace):
-            if t > 0:
-                rows = times(rows, at_pair) * (1.0 - gains[t : t + 1, :])
-            if (t + 1) % share == 0:
-                snap[(t + 1) // share - 1] = rows
+        rows = advance(rows, r * pace, (r + 1) * pace)
     get_b.wait()
     get_w2.wait()
     hidden = jax.nn.gelu(pre + b_v[...], approximate=True).astype(BF16)
@@ -103,30 +114,46 @@
 
     pl.semaphore_wait(barrier, total - 1)
 
-    def to_peer(step, source, target, send, recv):
-        peer = lax.rem(k + step, mp)
+    def remote(source, target, send, recv, c_to, k_to):
         return pltpu.make_async_remote_copy(
-            source, target, send.at[step], recv.at[step],
-            device_id={"tm": c, "mp": peer}, device_id_type=MESH,
+            source, target, send, recv, device_id={"tm": c_to, "mp": k_to}, device_id_type=MESH
         )
 
     def phi_copy(step):
         peer = lax.rem(k + step, mp)
-        return pltpu.make_async_remote_copy(
+        return remote(
             snap.at[lax.rem(peer + mp - 1, mp)], phi_all.at[k], phi_ss.at[step], phi_rs.at[step],
-            device_id={"tm": c, "mp": peer}, device_id_type=MESH,
-        )
-
-    part_copies = [to_peer(s, part.at[k], part.at[k], part_ss, part_rs) for s in range(1, mp)]
-    m_copies = [to_peer(s, snap.at[mp - 1], m_all.at[k], m_ss, m_rs) for s in range(1, mp)]
+            c, peer,
+        )
+
+    def in_set(step, source, target, send, recv):
+        peer = set_c * group + lax.rem(here + step, group)
+        return remote(source, target, send.at[step], recv.at[step], peer, k)
+
+    part_copies = [
+        remote(part.at[k], part.at[k], part_ss.at[s], part_rs.at[s], c, lax.rem(k + s, mp))
+        for s in range(1, mp)
+    ]
+    for copy in part_copies:
+        copy.start()
+    rows = advance(rows, pace * chunks, frames)
+
+    own = snap.at[mp - 1]
+    come = [lax.rem(here + group - s, group) for s in range(group)]
+    r1 = [in_set(s, own, m_all.at[here, k], r1_ss, r1_rs) for s in range(1, group)]
+    r2, r3, r4 = [], [], []
+    for s in range(group):
+        j = come[s]
+        mine = own if s == 0 else m_all.at[j, k]
+        r2.append(remote(mine, m_all.at[j, k], r2_ss.at[s], r2_rs.at[s], c, across))
+        r3.append(remote(mine, m_all.at[j, k], r3_ss.at[s], r3_rs.at[s], c, beside))
+        r4.append(
+            remote(m_all.at[j, across], m_all.at[j, across], r4_ss.at[s], r4_rs.at[s], c, beside)
+        )
     phi_copies = [phi_copy(s) for s in range(1, mp)]
-    for copy in part_copies:
-        copy.start()
-    for copy in m_copies:
-        copy.start()
-    for copy in phi_copies:
-        copy.start()
-    m_all[k] = snap[mp - 1]
+    for copy in r1 + r2[:1] + r3[:1]:
+        copy.start()
+    m_all[here, k] = snap[mp - 1]
     phi_all[k] = snap[lax.rem(k + mp - 1, mp)]
     get_off.wait()
     get_sg.wait()
@@ -148,32 +175,53 @@
             vel[pl.ds(t, 1), :] = state[0:1]
         return state
 
-    vel_end = lax.fori_loop(0, mp, pass_frames, jnp.zeros((8, grid), F32))
-    for copy in m_copies:
+    early = mp // 2
+    vel_end = lax.fori_loop(0, early, pass_frames, jnp.zeros((8, grid), F32))
+    for s in range(1, group):
+        r1[s - 1].wait_recv()
+        r2[s].start()
+        r3[s].start()
+    for copy in phi_copies:
+        copy.start()
+    vel_end = lax.fori_loop(early, mp, pass_frames, vel_end)
+    v_all[here] = vel_end
+    v_copies = [in_set(s, v_all.at[here], v_all.at[here], v_ss, v_rs) for s in range(1, group)]
+    for copy in v_copies:
+        copy.start()
+    for s in range(group):
+        r2[s].wait_recv()
+        r4[s].start()
+    for s in range(group):
+        r3[s].wait_recv()
+        r4[s].wait_recv()
+        store_split(m_pair.at[come[s]], m_all[come[s]].reshape(grid, grid))
+    for copy in v_copies:
         copy.wait_recv()
-    store_split(m_pair, m_all[...].reshape(grid, grid))
+
+    chain = remote(x_out, x_in, chain_ss, chain_rs, lax.rem(c + group, tm), k)
+
+    @pl.when(set_c == 0)
+    def _():
+        x_in[...] = jnp.zeros_like(x_in)
+
+    @pl.when(set_c > 0)
+    def _():
+        chain.wait_recv()
+
+    def whole_block(j, state):
+        return times(state, m_pair.at[j]) + v_all[j]
+
+    state = lax.fori_loop(0, here, whole_block, x_in[...])
+
+    @pl.when(set_c < sets - 1)
+    def _():
+        x_out[...] = lax.fori_loop(here, group, whole_block, state)
+        chain.start()
+
+    x_in[...] = state
     for copy in phi_copies:
         copy.wait_recv()
     store_split(phi_pair, phi_all[...].reshape(grid, grid))
-
-    chain = pltpu.make_async_remote_copy(
-        x_out, x_in, chain_ss, chain_rs,
-        device_id={"tm": lax.rem(c + 1, tm), "mp": k}, device_id_type=MESH,
-    )
-
-    @pl.when(c == 0)
-    def _():
-        x_in[...] = jnp.zeros_like(x_in)
-        x_out[...] = vel_end
-
-    @pl.when(c > 0)
-    def _():
-        chain.wait_recv()
-        x_out[...] = times(x_in[...], m_pair) + vel_end
-
-    @pl.when(c < tm - 1)
-    def _():
-        chain.start()
 
     @pl.when(k == 0)
     def _():
@@ -188,13 +236,15 @@
         state = frame(k * share + j, state)
         f8[j : j + 1, :] = state[0:1]
     filtered = f8[...]
-    filt_o[...] = filtered
+    packed[:share, :] = filtered
     last = jnp.where(place == total - 1, 0.0, 1.0).astype(F32)
     row = lax.broadcasted_iota(jnp.int32, (share, grid), 0)
     weight = sg[pl.ds(pl.multiple_of(k * share, share), share), :]
     weight = jnp.where(row == share - 1, weight * last, weight)
     e8[...] = weight
     u8[...] = filtered - weight * times(filtered, at_pair)
+    packed[share : 2 * share, :] = u8[...]
+    packed[2 * share : 3 * share, :] = weight
     slope = jnp.ones((1, grid), F32)
     value = jnp.zeros((1, grid), F32)
     for j in range(share - 1, -1, -1):
@@ -225,21 +275,28 @@
         return both[0:1] * later + both[1:2]
 
     later = lax.fori_loop(0, total - 1 - place, gather_back, jnp.zeros((1, grid), F32))
-    for j in range(share - 1, -1, -1):
-        later = u8[j : j + 1, :] + e8[j : j + 1, :] * later
-        smooth_o[j : j + 1, :] = later
+    packed[3 * share :, :] = jnp.broadcast_to(later, (8, grid))
 
     def end_back(other, carry):
         back_copy(other).wait_send()
         return carry
 
     lax.fori_loop(0, place, end_back, 0)
-    for copy in part_copies + m_copies + phi_copies:
+    for copy in part_copies + r1 + r2 + r3 + r4 + v_copies + phi_copies:
         copy.wait_send()
 
-    @pl.when(c < tm - 1)
+    @pl.when(set_c < sets - 1)
     def _():
         chain.wait_send()
+
+
+def finish(share, packed, filt_o, smooth_o):
+    filt_o[...] = packed[:share, :]
+    later = packed[3 * share : 3 * share + 1, :]
+    for j in range(share - 1, -1, -1):
+        fresh, weight = share + j, 2 * share + j
+        later = packed[fresh : fresh + 1, :] + packed[weight : weight + 1, :] * later
+        smooth_o[j : j + 1, :] = later
 
 
 def on_device(features, w_in, b_in, output_weight, offset, transition, gains, smooth_gains):
@@ -250,29 +307,31 @@
     share = frames // mp
     quarter = grid // mp
     chunks = 8
+    group = math.gcd(tm, GROUP)
     args = (
         features, w_in, b_in.reshape(1, units), output_weight, offset.reshape(1, grid),
         transition, gains, smooth_gains,
     )
     dma = pltpu.SemaphoreType.DMA
     out = jax.ShapeDtypeStruct((share, grid), F32)
-    return pl.pallas_call(
-        functools.partial(kernel, tm, mp, chunks),
-        out_shape=(out, out),
+    packed = pl.pallas_call(
+        functools.partial(kernel, tm, mp, chunks, group),
+        out_shape=jax.ShapeDtypeStruct((3 * share + 8, grid), F32),
         in_specs=[pl.BlockSpec(memory_space=pl.ANY)] * len(args),
-        out_specs=(pl.BlockSpec(memory_space=pltpu.VMEM),) * 2,
+        out_specs=pl.BlockSpec(memory_space=pltpu.VMEM),
         scratch_shapes=[pltpu.VMEM(a.shape, a.dtype) for a in args]
         + [
             pltpu.VMEM((grid, grid), F32),
             pltpu.VMEM((grid, 2 * grid), BF16),
-            pltpu.VMEM((grid, 2 * grid), BF16),
+            pltpu.VMEM((group, grid, 2 * grid), BF16),
             pltpu.VMEM((grid, 2 * grid), BF16),
             pltpu.VMEM((mp, frames, grid), F32),
             pltpu.VMEM((frames, grid), F32),
             pltpu.VMEM((mp, quarter, grid), F32),
-            pltpu.VMEM((mp, quarter, grid), F32),
+            pltpu.VMEM((group, mp, quarter, grid), F32),
             pltpu.VMEM((mp, quarter, grid), F32),
             pltpu.VMEM((frames, grid), F32),
+            pltpu.VMEM((group, 8, grid), F32),
             pltpu.VMEM((8, grid), F32),
             pltpu.VMEM((8, grid), F32),
             pltpu.VMEM((8, grid), F32),
@@ -282,13 +341,26 @@
             pltpu.VMEM((2, grid), F32),
             pltpu.VMEM((tm * mp, 2, grid), F32),
             dma((8 + chunks,)),
-            dma((mp,)), dma((mp,)), dma((mp,)), dma((mp,)), dma((mp,)), dma((mp,)),
+            dma((mp,)), dma((mp,)),
+            *[dma((group,))] * 8,
+            dma((mp,)), dma((mp,)),
+            dma((group,)), dma((group,)),
             dma(()), dma(()),
             dma((tm * mp,)), dma((tm * mp,)),
         ],
-        compiler_params=pltpu.CompilerParams(collective_id=0, has_side_effects=True),
+        compiler_params=pltpu.CompilerParams(
+            collective_id=0, has_side_effects=True
+        ),
         name="track",
     )(*args)
+    whole = pl.BlockSpec(memory_space=pltpu.VMEM)
+    return pl.pallas_call(
+        functools.partial(finish, share),
+        out_shape=(out, out),
+        in_specs=[whole],
+        out_specs=(whole, whole),
+        name="finish",
+    )(packed)
 
 
 def solution(mesh):

time: 49 us -> 34.7 us (0.71)
  Pallas kernels: 45.5 us -> 33.9 us
  local copies, waits for them, and re-layouts: 2.59 us -> 0 us
    pallas_call x1 -> x2, Pallas kernels: 45.5 us -> 33.9 us  [the longest x1 32.5 us: on_device(): pl.pallas_call(functools.partial(kernel, tm, mp, chunks, group), out_shap...]
    unnamed x2 -> x0, local copies, waits for them, and re-layouts: 2.59 us -> none
where the time goes in v2:
time: 34.7 us; the launch traced here: 34.6 us
  Pallas kernels  33.9 us (98%)
  between operations  0.64 us (2%)
    pallas_call x1, Pallas kernels, on_device(): pl.pallas_call(functools.partial(kernel, tm, mp, chunks, group), out_shap...  32.5 us
    pallas_call x1, Pallas kernels, on_device(): pl.pallas_call(functools.partial(finish, share), out_shape=(out, out), in...  1.38 us

profile of v2, /device:TPU:0, one launch (start us, length us, event | category | flops | bytes accessed | tf_op | source)
XLA Modules:
  0.0 34.6 jit_solution(6812475508862273519)
XLA Ops:
  0.6 32.5 %track.1.packed = f32[32,256]{1,0:T(8,128)} custom-call(bf16[32,2048]{1,0:T(8,128)(2,1)} %feat_h.1, bf16[2048,1024]{1,0:T(8,128)(2,1)} %w_in_h.1, f32[1,1024]{1,0:T(1,128)} %bitcast.2, bf16[1024,256]{1,0:T(8,128)(2,1)} %w2_h.1, f32[1,256]{1,0:T(1,128)} %bitcast.3, f32[256,256]{1,0:T(8,128)} %trans_h.1, f32[32,256]{1,0:T(8,128)} %gains_h.1, f32[32,256]{1,0:T(8,128)} %sg_h.1), custom_call_target="tpu_custom_call" | custom-call | tf_op jit(solution)/shard_map/track/pallas_call | solution.py:317
  33.2 1.4 %finish.1 = (f32[8,256]{1,0:T(8,128)}, f32[8,256]{1,0:T(8,128)}) custom-call(f32[32,256]{1,0:T(8,128)} %track.1.packed), custom_call_target="tpu_custom_call" | custom-call | tf_op jit(solution)/shard_map/finish/pallas_call | solution.py:357

commit v3 on v2

--- a/solution.py
+++ b/solution.py
@@ -26,6 +26,11 @@
     target[:, width:] = rest.astype(BF16)
 
 
+def store_product(target, quarters):
+    count, rows, grid = quarters.shape
+    store_split(target, quarters[...].reshape(count * rows, grid))
+
+
 def times(rows, pair):
     count, width = rows.shape
     both = jnp.concatenate(split(rows), 0).astype(BF16)
@@ -39,9 +44,9 @@
     packed,
     feat, w_in, b_v, w2, off, trans, gains, sg,
     at, at_pair, m_pair, phi_pair, part, meas, snap, m_all, phi_all, vel, v_all, x_in, x_out, x_own,
-    f8, u8, e8, comp, comps,
+    f8, u8, e8, slope_own, value_own, slopes, values, shares,
     in_sem, part_ss, part_rs, r1_ss, r1_rs, r2_ss, r2_rs, r3_ss, r3_rs, r4_ss, r4_rs,
-    phi_ss, phi_rs, v_ss, v_rs, chain_ss, chain_rs, back_ss, back_rs,
+    phi_ss, phi_rs, v_ss, v_rs, chain_ss, chain_rs, slope_ss, slope_rs, back_ss, back_rs,
 ):
     c, k = lax.axis_index("tm"), lax.axis_index("mp")
     place = c * mp + k
@@ -151,8 +156,20 @@
             remote(m_all.at[j, across], m_all.at[j, across], r4_ss.at[s], r4_rs.at[s], c, beside)
         )
     phi_copies = [phi_copy(s) for s in range(1, mp)]
-    for copy in r1 + r2[:1] + r3[:1]:
-        copy.start()
+    def need(reader, j):
+        return ((j < reader) | (set_c < sets - 1)) & ((set_c > 0) | (j > 0))
+
+    def when(condition, *actions):
+        @pl.when(condition)
+        def _():
+            for action in actions:
+                action()
+
+    wanted = [need(here, come[s]) for s in range(group)]
+    given = [need(lax.rem(here + s, group), here) for s in range(group)]
+    for s in range(1, group):
+        when(given[s], r1[s - 1].start)
+    when(wanted[0], r2[0].start, r3[0].start)
     m_all[here, k] = snap[mp - 1]
     phi_all[k] = snap[lax.rem(k + mp - 1, mp)]
     get_off.wait()
@@ -175,12 +192,10 @@
             vel[pl.ds(t, 1), :] = state[0:1]
         return state
 
-    early = mp // 2
+    early = 3 * mp // 4
     vel_end = lax.fori_loop(0, early, pass_frames, jnp.zeros((8, grid), F32))
     for s in range(1, group):
-        r1[s - 1].wait_recv()
-        r2[s].start()
-        r3[s].start()
+        when(wanted[s], r1[s - 1].wait_recv, r2[s].start, r3[s].start)
     for copy in phi_copies:
         copy.start()
     vel_end = lax.fori_loop(early, mp, pass_frames, vel_end)
@@ -188,13 +203,50 @@
     v_copies = [in_set(s, v_all.at[here], v_all.at[here], v_ss, v_rs) for s in range(1, group)]
     for copy in v_copies:
         copy.start()
+    last = jnp.where(place == total - 1, 0.0, 1.0).astype(F32)
+    row = lax.broadcasted_iota(jnp.int32, (share, grid), 0)
+    weight = sg[pl.ds(pl.multiple_of(k * share, share), share), :]
+    e8[...] = jnp.where(row == share - 1, weight * last, weight)
+    slope = e8[0:1, :]
+    for j in range(1, share):
+        slope = slope * e8[j : j + 1, :]
+    slope_own[...] = slope
+
+    def back_copy(own, target, send, recv, other):
+        return remote(
+            own, target.at[place], send.at[other], recv.at[place], other // mp, lax.rem(other, mp)
+        )
+
+    def from_later(own, target, send, recv, source):
+        return remote(
+            own, target.at[source], send.at[source], recv.at[source],
+            source // mp, lax.rem(source, mp),
+        )
+
+    to_slopes = (slope_own, slopes, slope_ss, slope_rs)
+    to_values = (value_own, values, back_ss, back_rs)
+
+    def send_slope(other, carry):
+        back_copy(*to_slopes, other).start()
+        return carry
+
+    def send_value(other, carry):
+        back_copy(*to_values, other).start()
+        return carry
+
+    lax.fori_loop(0, place, send_slope, 0)
     for s in range(group):
-        r2[s].wait_recv()
-        r4[s].start()
+        when(wanted[s], r2[s].wait_recv, r4[s].start)
     for s in range(group):
-        r3[s].wait_recv()
-        r4[s].wait_recv()
-        store_split(m_pair.at[come[s]], m_all[come[s]].reshape(grid, grid))
+        when(
+            wanted[s], r3[s].wait_recv, r4[s].wait_recv,
+            functools.partial(store_product, m_pair.at[come[s]], m_all.at[come[s]]),
+        )
+
+    @pl.when(set_c == 0)
+    def _():
+        m_pair[0] = jnp.zeros_like(m_pair[0])
+
     for copy in v_copies:
         copy.wait_recv()
 
@@ -204,9 +256,8 @@
     def _():
         x_in[...] = jnp.zeros_like(x_in)
 
-    @pl.when(set_c > 0)
-    def _():
-        chain.wait_recv()
+    keep_phi = functools.partial(store_product, phi_pair, phi_all)
+    when(set_c > 0, *[copy.wait_recv for copy in phi_copies], keep_phi, chain.wait_recv)
 
     def whole_block(j, state):
         return times(state, m_pair.at[j]) + v_all[j]
@@ -219,9 +270,7 @@
         chain.start()
 
     x_in[...] = state
-    for copy in phi_copies:
-        copy.wait_recv()
-    store_split(phi_pair, phi_all[...].reshape(grid, grid))
+    when(set_c == 0, *[copy.wait_recv for copy in phi_copies], keep_phi)
 
     @pl.when(k == 0)
     def _():
@@ -237,53 +286,41 @@
         f8[j : j + 1, :] = state[0:1]
     filtered = f8[...]
     packed[:share, :] = filtered
-    last = jnp.where(place == total - 1, 0.0, 1.0).astype(F32)
-    row = lax.broadcasted_iota(jnp.int32, (share, grid), 0)
-    weight = sg[pl.ds(pl.multiple_of(k * share, share), share), :]
-    weight = jnp.where(row == share - 1, weight * last, weight)
-    e8[...] = weight
+    weight = e8[...]
     u8[...] = filtered - weight * times(filtered, at_pair)
+    value = u8[share - 1 : share, :]
+    for j in range(share - 2, -1, -1):
+        value = u8[j : j + 1, :] + e8[j : j + 1, :] * value
+    value_own[...] = value
+    lax.fori_loop(0, place, send_value, 0)
     packed[share : 2 * share, :] = u8[...]
     packed[2 * share : 3 * share, :] = weight
-    slope = jnp.ones((1, grid), F32)
-    value = jnp.zeros((1, grid), F32)
-    for j in range(share - 1, -1, -1):
-        slope = slope * e8[j : j + 1, :]
-        value = u8[j : j + 1, :] + e8[j : j + 1, :] * value
-    comp[0:1, :] = slope
-    comp[1:2, :] = value
-
-    def back_copy(other):
-        return pltpu.make_async_remote_copy(
-            comp, comps.at[place], back_ss.at[other], back_rs.at[place],
-            device_id={"tm": other // mp, "mp": lax.rem(other, mp)}, device_id_type=MESH,
-        )
-
-    def send_back(step, carry):
-        back_copy(place - 1 - step).start()
+
+    def weigh(source, part):
+        from_later(*to_slopes, source).wait_recv()
+        shares[source] = part
+        return part * slopes[source]
+
+    def add_up(source, later):
+        from_later(*to_values, source).wait_recv()
+        return later + shares[source] * values[source]
+
+    lax.fori_loop(place + 1, total, weigh, jnp.ones((1, grid), F32))
+    later = lax.fori_loop(place + 1, total, add_up, jnp.zeros((1, grid), F32))
+    packed[3 * share :, :] = jnp.broadcast_to(later, (8, grid))
+
+    def end_back(other, carry):
+        back_copy(*to_slopes, other).wait_send()
+        back_copy(*to_values, other).wait_send()
         return carry
 
-    lax.fori_loop(0, place, send_back, 0)
-
-    def gather_back(step, later):
-        source = total - 1 - step
-        pltpu.make_async_remote_copy(
-            comp, comps.at[source], back_ss.at[source], back_rs.at[source],
-            device_id={"tm": source // mp, "mp": lax.rem(source, mp)}, device_id_type=MESH,
-        ).wait_recv()
-        both = comps[source]
-        return both[0:1] * later + both[1:2]
-
-    later = lax.fori_loop(0, total - 1 - place, gather_back, jnp.zeros((1, grid), F32))
-    packed[3 * share :, :] = jnp.broadcast_to(later, (8, grid))
-
-    def end_back(other, carry):
-        back_copy(other).wait_send()
-        return carry
-
     lax.fori_loop(0, place, end_back, 0)
-    for copy in part_copies + r1 + r2 + r3 + r4 + v_copies + phi_copies:
+    for copy in part_copies + v_copies + phi_copies:
         copy.wait_send()
+    for s in range(group):
+        if s > 0:
+            when(given[s], r1[s - 1].wait_send)
+        when(wanted[s], r2[s].wait_send, r3[s].wait_send, r4[s].wait_send)
 
     @pl.when(set_c < sets - 1)
     def _():
@@ -338,15 +375,18 @@
             pltpu.VMEM((share, grid), F32),
             pltpu.VMEM((share, grid), F32),
             pltpu.VMEM((share, grid), F32),
-            pltpu.VMEM((2, grid), F32),
-            pltpu.VMEM((tm * mp, 2, grid), F32),
+            pltpu.VMEM((1, grid), F32),
+            pltpu.VMEM((1, grid), F32),
+            pltpu.VMEM((tm * mp, 1, grid), F32),
+            pltpu.VMEM((tm * mp, 1, grid), F32),
+            pltpu.VMEM((tm * mp, 1, grid), F32),
             dma((8 + chunks,)),
             dma((mp,)), dma((mp,)),
             *[dma((group,))] * 8,
             dma((mp,)), dma((mp,)),
             dma((group,)), dma((group,)),
             dma(()), dma(()),
-            dma((tm * mp,)), dma((tm * mp,)),
+            *[dma((tm * mp,))] * 4,
         ],
         compiler_params=pltpu.CompilerParams(
             collective_id=0, has_side_effects=True

time: 34.7 us -> 34.1 us (0.983)
  Pallas kernels: 33.9 us -> 33.3 us
    pallas_call x1, Pallas kernels: 32.5 us -> 31.9 us  [on_device(): pl.pallas_call(functools.partial(kernel, tm, mp, chunks, group), out_shap...]
where the time goes in v3:
time: 34.1 us; the launch traced here: 33.9 us
  Pallas kernels  33.3 us (98%)
  between operations  0.64 us (2%)
    pallas_call x1, Pallas kernels, on_device(): pl.pallas_call(functools.partial(kernel, tm, mp, chunks, group), out_shap...  31.9 us
    pallas_call x1, Pallas kernels, on_device(): pl.pallas_call(functools.partial(finish, share), out_shape=(out, out), in...  1.38 us

profile of v3, /device:TPU:0, one launch (start us, length us, event | category | flops | bytes accessed | tf_op | source)
XLA Modules:
  0.0 33.9 jit_solution(14100407830173643698)
XLA Ops:
  0.6 31.9 %track.1.packed = f32[32,256]{1,0:T(8,128)} custom-call(bf16[32,2048]{1,0:T(8,128)(2,1)} %feat_h.1, bf16[2048,1024]{1,0:T(8,128)(2,1)} %w_in_h.1, f32[1,1024]{1,0:T(1,128)} %bitcast.2, bf16[1024,256]{1,0:T(8,128)(2,1)} %w2_h.1, f32[1,256]{1,0:T(1,128)} %bitcast.3, f32[256,256]{1,0:T(8,128)} %trans_h.1, f32[32,256]{1,0:T(8,128)} %gains_h.1, f32[32,256]{1,0:T(8,128)} %sg_h.1), custom_call_target="tpu_custom_call" | custom-call | tf_op jit(solution)/shard_map/track/pallas_call | solution.py:354
  32.6 1.4 %finish.1 = (f32[8,256]{1,0:T(8,128)}, f32[8,256]{1,0:T(8,128)}) custom-call(f32[32,256]{1,0:T(8,128)} %track.1.packed), custom_call_target="tpu_custom_call" | custom-call | tf_op jit(solution)/shard_map/finish/pallas_call | solution.py:397
